TPU v7x, 32 devices: a whole 2x2x4 slice. The times are simulated.
32 devices in a mesh: island: 4 (over y, core), shard: 8 (over z, x).
Axes of the slice: x: 2, y: 2, z: 4, core: 2. Of those that a mesh axis runs over, the one named last changes fastest.
Arguments:
- pseudo_grad: float32 [4, 2048, 4096], P('island', 'shard'), may hold values from -6 to 6
- error_buffer: float32 [4, 2048, 4096], P('island', 'shard'), may hold values from -6 to 6
- momentum: float32 [2048, 4096], P('shard'), may hold values from -4 to 4
- weights: bfloat16 [2048, 4096], P('shard'), may hold values from -6 to 6
- warm_basis: float32 [2048, 64], P('shard'), may hold values from -6 to 6
Outputs:
- new_error: float32 [4, 2048, 4096], P('island', 'shard')
- new_momentum: float32 [2048, 4096], P('shard')
- new_weights: bfloat16 [2048, 4096], P('shard')
- new_basis: float32 [2048, 64], P('shard')
All inputs are finite; a program needn't handle non-finite values.
Results may differ from a plain program's by a relative error of at most 0.001.
Values sent between devices are 32-bit elements; how exact they have to be, the bound alone decides.
A program may use at most 128 MiB of HBM per device.

v0:
```python
import jax
import jax.numpy as jnp
from jax import lax
from jax.sharding import PartitionSpec as P

ITERS = 2
HIGH = lax.Precision.HIGHEST
outer_beta = 0.9
outer_rate = 0.7


def orthonormal(factor_rows):
    gram_matrix = jnp.dot(factor_rows, factor_rows.T, precision=HIGH)
    lower_factor = jnp.linalg.cholesky(gram_matrix)
    return lax.linalg.triangular_solve(lower_factor, factor_rows, left_side=True, lower=True)


def on_device(pseudo_grad, error_buffer, momentum, weights, warm_basis):
    merged = (pseudo_grad + error_buffer)[0]
    basis_now = warm_basis
    for iteration in range(ITERS):
        partial_value = lax.dot_general(basis_now, merged, (((0,), (0,)), ((), ())), precision=HIGH)
        factor_rows = orthonormal(lax.psum(partial_value, ("island", "shard")))
        local_proj = lax.dot_general(merged, factor_rows, (((1,), (1,)), ((), ())), precision=HIGH)
        basis_now = lax.psum(local_proj, "island")
    new_error = merged - jnp.dot(local_proj, factor_rows, precision=HIGH)
    update = jnp.dot(basis_now / lax.axis_size("island"), factor_rows, precision=HIGH)
    new_momentum = outer_beta * momentum + update
    stepped = weights.astype(jnp.float32) - outer_rate * (update + outer_beta * new_momentum)
    return (new_error[None], new_momentum, stepped.astype(jnp.bfloat16), basis_now)


def solution(mesh):
    in_specs = (
        P("island", "shard", None),
        P("island", "shard", None),
        P("shard", None),
        P("shard", None),
        P("shard", None),
    )
    out_specs = (P("island", "shard", None), P("shard", None), P("shard", None), P("shard", None))
    return jax.shard_map(
        on_device, mesh=mesh, in_specs=in_specs, out_specs=out_specs, check_vma=False
    )
```

profile of v0, /device:TPU:0, one launch (start us, length us, event | category | flops | bytes accessed | tf_op | source)
XLA Modules:
  0.0 420.1 jit_solution(8857783116008560494)
XLA Ops:
  7.2 0.0 copy-start
  7.2 0.0 all-reduce.5.cloned.1.call-start
  7.2 3.9 add.25
  11.2 0.0 copy-start.1
  11.2 2.0 copy-done.1
  13.2 0.0 copy-done
  13.2 3.8 convolution_bitcast_fusion
  17.0 0.0 all-reduce.5.cloned.1.call-update
  17.0 0.0 all-reduce.7.cloned.1.call-start
  17.1 133.6 %all-reduce.5.cloned.1.call-done = f32[64,4096]{1,0:T(8,128)} async-done(((f32[64,4096]{1,0:T(8,128)}), f32[64,4096]{1,0:T(8,128)}) %all-reduce.5.cloned.1.call-update) | async-done | bytes 1048592 | tf_op jit(solution)/shard_map/psum | solution.py:23
  150.7 2.5 fusion.22
  153.3 0.1 copy.9
  153.3 5.8 %cholesky.44 = f32[64,64]{1,0:T(8,128)S(1)} custom-call(f32[64,64]{1,0:T(8,128)S(1)} %fusion.17), custom_call_target="Cholesky" | custom-call | tf_op jit(solution)/shard_map/jit(cholesky)/cholesky | solution.py:14
  159.2 0.6 compare_reduce_fusion.1
  159.9 0.7 fusion.10
  160.5 4.9 %custom-call.6 = f32[1,64,64]{1,2,0:T(8,128)S(1)} custom-call(f32[1,64,64]{2,1,0:T(8,128)S(1)} %fusion.10), custom_call_target="InvertDiagBlocksLowerTriangular" | custom-call | tf_op jit(solution)/shard_map/triangular_solve/custom-call.0 | solution.py:15
  165.4 2.3 fusion.15
  167.7 5.8 %fusion.5 = f32[256,64]{1,0:T(8,128)} fusion(f32[64,4096]{1,0:T(8,128)S(1)} %fusion.15, f32[1,256,4096]{2,1,0:T(8,128)} %copy-done.1), kind=kOutput, calls=%fused_computation.7 | convolution fusion | flops 805306368 | bytes 5308416 | tf_op jit(solution)/shard_map/dot_general | solution.py:24
  173.5 0.0 all-reduce.7.cloned.1.call-update
  173.6 0.2 all-reduce.9.cloned.1.call-start
  173.8 30.7 %all-reduce.7.cloned.1.call-done = f32[256,64]{1,0:T(8,128)} async-done(((f32[256,64]{1,0:T(8,128)}), f32[256,64]{1,0:T(8,128)}) %all-reduce.7.cloned.1.call-update) | async-done | bytes 65552 | tf_op jit(solution)/shard_map/psum | solution.py:25
  204.4 5.9 %fusion.3 = f32[64,4096]{1,0:T(8,128)} fusion(f32[256,64]{1,0:T(8,128)} %all-reduce.7.cloned.1.call-done, f32[1,256,4096]{2,1,0:T(8,128)} %copy-done.1), kind=kOutput, calls=%fused_computation.5 | convolution fusion | flops 805306368 | bytes 5308416 | tf_op jit(solution)/shard_map/dot_general | solution.py:22
  210.3 0.0 all-reduce.9.cloned.1.call-update
  210.3 130.9 %all-reduce.9.cloned.1.call-done = f32[64,4096]{1,0:T(8,128)} async-done(((f32[64,4096]{1,0:T(8,128)}), f32[64,4096]{1,0:T(8,128)}) %all-reduce.9.cloned.1.call-update) | async-done | bytes 1048592 | tf_op jit(solution)/shard_map/psum | solution.py:23
  341.2 2.5 fusion.23
  343.8 0.1 copy.10
  343.9 5.8 %cholesky.55 = f32[64,64]{1,0:T(8,128)S(1)} custom-call(f32[64,64]{1,0:T(8,128)S(1)} %fusion.14), custom_call_target="Cholesky" | custom-call | tf_op jit(solution)/shard_map/jit(cholesky)/cholesky | solution.py:14
  349.7 0.6 compare_reduce_fusion
  350.4 0.7 fusion.11
  351.1 4.9 %custom-call.7 = f32[1,64,64]{1,2,0:T(8,128)S(1)} custom-call(f32[1,64,64]{2,1,0:T(8,128)S(1)} %fusion.11), custom_call_target="InvertDiagBlocksLowerTriangular" | custom-call | tf_op jit(solution)/shard_map/triangular_solve/custom-call.0 | solution.py:15
  355.9 2.3 fusion.12
  358.2 6.1 %fusion.1 = f32[256,64]{0,1:T(8,128)S(1)} fusion(f32[64,4096]{1,0:T(8,128)S(1)} %fusion.12, f32[1,256,4096]{2,1,0:T(8,128)} %copy-done.1), kind=kOutput, calls=%fused_computation.3 | convolution fusion | flops 805306368 | bytes 5308416 | tf_op jit(solution)/shard_map/dot_general | solution.py:24
  364.3 0.0 copy-start.3
  364.3 0.0 copy-start.2
  364.4 6.8 %fusion = f32[1,256,4096]{2,1,0:T(8,128)} fusion(f32[256,64]{0,1:T(8,128)S(1)} %fusion.1, f32[64,4096]{1,0:T(8,128)S(1)} %fusion.12, f32[1,256,4096]{2,1,0:T(8,128)} %copy-done.1), kind=kOutput, calls=%fused_computation.1 | convolution fusion | flops 806354944 | bytes 9502720 | tf_op jit(solution)/shard_map/dot_general | solution.py:26
  371.1 0.0 copy-done.3
  371.1 0.0 all-reduce.11.cloned.1.call-start
  371.1 0.6 all-reduce.11.cloned.1.call-update
  371.7 33.3 %all-reduce.11.cloned.1.call-done = f32[256,64]{0,1:T(8,128)} async-done(((f32[256,64]{0,1:T(8,128)}), f32[256,64]{0,1:T(8,128)}) %all-reduce.11.cloned.1.call-update) | async-done | bytes 65552 | tf_op jit(solution)/shard_map/psum | solution.py:25
  405.0 0.0 copy-done.2
  405.0 0.0 copy-start.4
  405.0 7.9 %subtract_convert_fusion = (bf16[256,4096]{1,0:T(8,128)(2,1)}, f32[256,4096]{1,0:T(8,128)}) fusion(bf16[256,4096]{1,0:T(8,128)(2,1)S(1)} %copy-done.2, f32[256,4096]{1,0:T(8,128)} %param.10, f32[64,4096]{1,0:T(8,128)S(1)} %fusion.12, f32[256,64]{0,1:T(8,128)} %all-reduce.11.cloned.1.call-done), kind=kOutput, calls=%fused_computation.10 | convolution fusion | flops 813711360 | bytes 13697024 | tf_op jit(solution)/shard_map/dot_general | solution.py:27
  412.9 0.0 copy-done.4
  412.9 0.6 copy.15
  (4 shorter events, 0.1 us)
Async XLA Ops:
  7.2 6.0 %copy-start = (f32[256,64]{0,1:T(8,128)S(1)}, f32[256,64]{0,1:T(8,128)}, u32[]{:S(2)}) copy-start(f32[256,64]{0,1:T(8,128)} %param.12) | copy-start | bytes 196612
  7.2 143.5 %all-reduce.5.cloned.1.call-start = ((), (), s32[]{:S(2)}) async-start(), calls=%async_computation | async-start | bytes 2097152 | tf_op jit(solution)/shard_map/psum | solution.py:23
  11.2 2.0 copy-start.1
  17.0 187.4 %all-reduce.7.cloned.1.call-start = ((), (), s32[]{:S(2)}) async-start(), calls=%async_computation.1 | async-start | bytes 262144 | tf_op jit(solution)/shard_map/psum | solution.py:25
  173.6 167.7 %all-reduce.9.cloned.1.call-start = ((), (), s32[]{:S(2)}) async-start(), calls=%async_computation.2 | async-start | bytes 2097152 | tf_op jit(solution)/shard_map/psum | solution.py:23
  364.3 6.8 %copy-start.3 = (f32[256,64]{0,1:T(8,128)}, f32[256,64]{0,1:T(8,128)S(1)}, u32[]{:S(2)}) copy-start(f32[256,64]{0,1:T(8,128)S(1)} %fusion.1) | copy-start | bytes 196612
  364.3 40.7 %copy-start.2 = (bf16[256,4096]{1,0:T(8,128)(2,1)S(1)}, bf16[256,4096]{1,0:T(8,128)(2,1)}, u32[]{:S(2)}) copy-start(bf16[256,4096]{1,0:T(8,128)(2,1)} %param.11) | copy-start | bytes 6291460
  371.1 33.9 %all-reduce.11.cloned.1.call-start = ((), (), s32[]{:S(2)}) async-start(), calls=%async_computation.3 | async-start | bytes 131072 | tf_op jit(solution)/shard_map/psum | solution.py:25
  405.0 7.9 %copy-start.4 = (f32[256,64]{0,1:T(8,128)S(1)}, f32[256,64]{0,1:T(8,128)}, u32[]{:S(2)}) copy-start(f32[256,64]{0,1:T(8,128)} %all-reduce.11.cloned.1.call-done) | copy-start | bytes 196612
Sparse Core Ops, SparseCore 0:
  17.2 133.5 all-reduce.4
  173.7 30.7 all-reduce.6
  210.5 130.7 all-reduce.8
  374.5 30.4 all-reduce.10
where the time goes:
time: 420 us
  waiting for transfers between devices  329 us (78%)
  matrix products  45.8 us (11%)
  other arithmetic  28.1 us (7%)
  between operations  13.9 us (3%)
    psum x2, waiting for transfers between devices, on_device(): factor_rows = orthonormal(lax.psum(partial_value, ('island', 'shard')))  265 us
    psum x2, waiting for transfers between devices, on_device(): basis_now = lax.psum(local_proj, 'island')  64 us
    another operation x6, other arithmetic, orthonormal(): lower_factor = jnp.linalg.cholesky(gram_matrix)  13 us
    dot_general x2, matrix products, on_device(): lax.dot_general(merged, factor_rows, (((1,), (1,)), ((), ())), precision=...  11.9 us
    another operation x4, other arithmetic, orthonormal(): lax.linalg.triangular_solve(lower_factor, factor_rows, left_side=True, lo...  11.1 us
    dot_general x2, matrix products, on_device(): lax.dot_general(basis_now, merged, (((0,), (0,)), ((), ())), precision=HIGH)  9.69 us
  transfers between devices with their start and end apart: 4, of which 4 were waited for; matrix products, arithmetic and copies ran while one was open for 0% of the time, Pallas kernels for 0%

commit v1 on v0

--- a/solution.py
+++ b/solution.py
@@ -22,7 +22,13 @@
         partial_value = lax.dot_general(basis_now, merged, (((0,), (0,)), ((), ())), precision=HIGH)
         factor_rows = orthonormal(lax.psum(partial_value, ("island", "shard")))
         local_proj = lax.dot_general(merged, factor_rows, (((1,), (1,)), ((), ())), precision=HIGH)
-        basis_now = lax.psum(local_proj, "island")
+        size = lax.axis_size("island")
+        basis_now, hop = (local_proj, 1)
+        while hop < size:
+            basis_now = basis_now + lax.ppermute(
+                basis_now, "island", [(i, i ^ hop) for i in range(size)]
+            )
+            hop = 2 * hop
     new_error = merged - jnp.dot(local_proj, factor_rows, precision=HIGH)
     update = jnp.dot(basis_now / lax.axis_size("island"), factor_rows, precision=HIGH)
     new_momentum = outer_beta * momentum + update

time: 420 us -> 358 us (0.85)
  waiting for transfers between devices: 329 us -> 268 us
  matrix products: 45.8 us -> 41.2 us
    psum x2 -> x0, waiting for transfers between devices: 64 us -> none  [on_device(): basis_now = lax.psum(local_proj, 'island')]
    ppermute x0 -> x4, waiting for transfers between devices: none -> 5.32 us  [on_device(): lax.ppermute(basis_now, 'island', [(i, i ^ hop) for i in range(size)])]
  transfers between devices with their start and end apart: 4 -> 6, of which waited for: 4 -> 5; matrix products, arithmetic and copies ran while one was open for 0% -> 1% of each run, Pallas kernels for 0% -> 0%
where the time goes in v1:
time: 358 us
  waiting for transfers between devices  268 us (75%)
  matrix products  41.2 us (12%)
  other arithmetic  28.1 us (8%)
  between operations  14.2 us (4%)
    psum x2, waiting for transfers between devices, on_device(): factor_rows = orthonormal(lax.psum(partial_value, ('island', 'shard')))  263 us
    another operation x6, other arithmetic, orthonormal(): lower_factor = jnp.linalg.cholesky(gram_matrix)  13 us
    dot_general x2, matrix products, on_device(): lax.dot_general(merged, factor_rows, (((1,), (1,)), ((), ())), precision=...  12.2 us
    another operation x4, other arithmetic, orthonormal(): lax.linalg.triangular_solve(lower_factor, factor_rows, left_side=True, lo...  11.1 us
    dot_general x2, matrix products, on_device(): lax.dot_general(basis_now, merged, (((0,), (0,)), ((), ())), precision=HIGH)  7.43 us
  transfers between devices with their start and end apart: 6, of which 5 were waited for; matrix products, arithmetic and copies ran while one was open for 1% of the time, Pallas kernels for 0%

profile of v1, /device:TPU:0, one launch (start us, length us, event | category | flops | bytes accessed | tf_op | source)
XLA Modules:
  0.0 357.6 jit_solution(14821967077679782719)
XLA Ops:
  7.2 0.0 copy-start
  7.2 0.0 all-reduce.3.cloned.1.call-start
  7.2 3.9 %add.33 = f32[1,256,4096]{2,1,0:T(8,128)S(1)} add(f32[1,256,4096]{2,1,0:T(8,128)} %param.8, f32[1,256,4096]{2,1,0:T(8,128)} %param.9) | non-fusion elementwise | flops 1048576 | bytes 12582912 | tf_op jit(solution)/shard_map/add | solution.py:19
  11.2 0.0 copy-start.1
  11.2 2.0 copy-done.1
  13.2 0.0 copy-done
  13.2 3.8 %convolution_bitcast_fusion = f32[64,4096]{1,0:T(8,128)} fusion(f32[256,64]{0,1:T(8,128)S(1)} %copy-done, f32[1,256,4096]{2,1,0:T(8,128)S(1)} %add.33), kind=kOutput, calls=%fused_computation.2 | convolution fusion | flops 805306368 | bytes 5308416 | tf_op jit(solution)/shard_map/dot_general | solution.py:22
  17.0 0.0 all-reduce.3.cloned.1.call-update
  17.0 0.2 all-reduce.5.cloned.1.call-start
  17.3 133.3 %all-reduce.3.cloned.1.call-done = f32[64,4096]{1,0:T(8,128)} async-done(((f32[64,4096]{1,0:T(8,128)}), f32[64,4096]{1,0:T(8,128)}) %all-reduce.3.cloned.1.call-update) | async-done | bytes 1048592 | tf_op jit(solution)/shard_map/psum | solution.py:23
  150.6 2.5 fusion.23
  153.1 0.1 copy.9
  153.2 5.8 %cholesky.44 = f32[64,64]{1,0:T(8,128)S(1)} custom-call(f32[64,64]{1,0:T(8,128)S(1)} %fusion.18), custom_call_target="Cholesky" | custom-call | tf_op jit(solution)/shard_map/jit(cholesky)/cholesky | solution.py:14
  159.1 0.6 compare_reduce_fusion.1
  159.7 0.7 fusion.11
  160.4 4.9 %custom-call.6 = f32[1,64,64]{1,2,0:T(8,128)S(1)} custom-call(f32[1,64,64]{2,1,0:T(8,128)S(1)} %fusion.11), custom_call_target="InvertDiagBlocksLowerTriangular" | custom-call | tf_op jit(solution)/shard_map/triangular_solve/custom-call.0 | solution.py:15
  165.3 0.0 copy-start.2
  165.3 2.4 fusion.16
  167.7 6.1 %fusion.5 = f32[256,64]{0,1:T(8,128)S(1)} fusion(f32[64,4096]{1,0:T(8,128)S(1)} %fusion.16, f32[1,256,4096]{2,1,0:T(8,128)} %copy-done.1), kind=kOutput, calls=%fused_computation.7 | convolution fusion | flops 805306368 | bytes 5308416 | tf_op jit(solution)/shard_map/dot_general | solution.py:24
  173.9 0.1 collective-permute-start
  173.9 1.2 collective-permute-done
  175.2 1.5 collective-permute-start.1
  176.7 2.8 collective-permute-done.1
  179.5 0.0 copy-done.2
  179.5 3.6 %fusion.3 = f32[64,4096]{1,0:T(8,128)} fusion(f32[1,256,4096]{2,1,0:T(8,128)S(1)} %copy-done.2, f32[256,64]{0,1:T(8,128)S(1)} %add.34, f32[256,64]{0,1:T(8,128)S(1)} %collective-permute-done.1), kind=kOutput, calls=%fused_computation.5 | convolution fusion | flops 805322752 | bytes 5373952 | tf_op jit(solution)/shard_map/dot_general | solution.py:22
  183.1 0.0 all-reduce.5.cloned.1.call-update
  183.1 129.8 %all-reduce.5.cloned.1.call-done = f32[64,4096]{1,0:T(8,128)} async-done(((f32[64,4096]{1,0:T(8,128)}), f32[64,4096]{1,0:T(8,128)}) %all-reduce.5.cloned.1.call-update) | async-done | bytes 1048592 | tf_op jit(solution)/shard_map/psum | solution.py:23
  312.9 2.5 fusion.24
  315.5 0.1 copy.10
  315.5 5.8 %cholesky.55 = f32[64,64]{1,0:T(8,128)S(1)} custom-call(f32[64,64]{1,0:T(8,128)S(1)} %fusion.15), custom_call_target="Cholesky" | custom-call | tf_op jit(solution)/shard_map/jit(cholesky)/cholesky | solution.py:14
  321.4 0.6 compare_reduce_fusion
  322.1 0.7 fusion.12
  322.7 4.9 %custom-call.7 = f32[1,64,64]{1,2,0:T(8,128)S(1)} custom-call(f32[1,64,64]{2,1,0:T(8,128)S(1)} %fusion.12), custom_call_target="InvertDiagBlocksLowerTriangular" | custom-call | tf_op jit(solution)/shard_map/triangular_solve/custom-call.0 | solution.py:15
  327.6 0.0 copy-start.3
  327.6 2.6 fusion.13
  330.3 6.1 %fusion.1 = f32[256,64]{0,1:T(8,128)S(1)} fusion(f32[64,4096]{1,0:T(8,128)S(1)} %fusion.13, f32[1,256,4096]{2,1,0:T(8,128)} %copy-done.1), kind=kOutput, calls=%fused_computation.3 | convolution fusion | flops 805306368 | bytes 5308416 | tf_op jit(solution)/shard_map/dot_general | solution.py:24
  336.4 0.1 collective-permute-start.2
  336.5 1.2 collective-permute-done.2
  337.7 0.0 copy-start.4
  337.8 0.0 copy-start.5
  337.8 1.5 collective-permute-start.3
  339.3 0.0 copy-done.3
  339.3 5.1 %fusion = f32[1,256,4096]{2,1,0:T(8,128)} fusion(f32[256,64]{0,1:T(8,128)S(1)} %fusion.1, f32[64,4096]{1,0:T(8,128)S(1)} %fusion.13, f32[1,256,4096]{2,1,0:T(8,128)S(1)} %copy-done.3), kind=kOutput, calls=%fused_computation.1 | convolution fusion | flops 806354944 | bytes 9502720 | tf_op jit(solution)/shard_map/dot_general | solution.py:32
  344.4 0.0 collective-permute-done.3
  344.4 0.0 copy-done.4
  344.4 0.0 copy-done.5
  344.4 0.0 copy-start.6
  344.4 6.4 %subtract_convert_fusion = (bf16[256,4096]{1,0:T(8,128)(2,1)}, f32[256,4096]{1,0:T(8,128)}) fusion(bf16[256,4096]{1,0:T(8,128)(2,1)S(1)} %copy-done.5, f32[256,4096]{1,0:T(8,128)S(1)} %copy-done.4, f32[64,4096]{1,0:T(8,128)S(1)} %fusion.13, f32[256,64]{0,1:T(8,128)S(1)} %add.37), kind=kOutput, calls=%fused_computation.10 | convolution fusion | flops 813711360 | bytes 13697024 | tf_op jit(solution)/shard_map/dot_general | solution.py:33
  (8 shorter events, 0.1 us)
Async XLA Ops:
  7.2 6.0 %copy-start = (f32[256,64]{0,1:T(8,128)S(1)}, f32[256,64]{0,1:T(8,128)}, u32[]{:S(2)}) copy-start(f32[256,64]{0,1:T(8,128)} %param.12) | copy-start | bytes 196612
  7.2 143.4 %all-reduce.3.cloned.1.call-start = ((), (), s32[]{:S(2)}) async-start(), calls=%async_computation | async-start | bytes 2097152 | tf_op jit(solution)/shard_map/psum | solution.py:23
  11.2 2.0 copy-start.1
  17.0 295.9 %all-reduce.5.cloned.1.call-start = ((), (), s32[]{:S(2)}) async-start(), calls=%async_computation.1 | async-start | bytes 2097152 | tf_op jit(solution)/shard_map/psum | solution.py:23
  165.3 14.2 %copy-start.2 = (f32[1,256,4096]{2,1,0:T(8,128)S(1)}, f32[1,256,4096]{2,1,0:T(8,128)}, u32[]{:S(2)}) copy-start(f32[1,256,4096]{2,1,0:T(8,128)} %copy-done.1) | copy-start | bytes 12582916
  173.9 1.3 collective-permute-start
  175.2 4.3 %collective-permute-start.1 = (f32[256,64]{0,1:T(8,128)S(1)}, f32[256,64]{0,1:T(8,128)S(1)}, u32[]{:S(2)}, u32[]{:S(2)}) collective-permute-start(f32[256,64]{0,1:T(8,128)S(1)} %add.34), channel_id=1, source_target_pairs={{0,16},{8,24},{16,0},{24,8},{1,17},{9,25},{17,1},{25,9},{2,18},{10... | collective-permute-start | bytes 196616 | tf_op jit(solution)/shard_map/ppermute | solution.py:28
  327.6 11.6 %copy-start.3 = (f32[1,256,4096]{2,1,0:T(8,128)S(1)}, f32[1,256,4096]{2,1,0:T(8,128)}, u32[]{:S(2)}) copy-start(f32[1,256,4096]{2,1,0:T(8,128)} %copy-done.1) | copy-start | bytes 12582916
  336.4 1.3 collective-permute-start.2
  337.7 6.7 %copy-start.4 = (f32[256,4096]{1,0:T(8,128)S(1)}, f32[256,4096]{1,0:T(8,128)}, u32[]{:S(2)}) copy-start(f32[256,4096]{1,0:T(8,128)} %param.10) | copy-start | bytes 12582916
  337.8 6.7 %copy-start.5 = (bf16[256,4096]{1,0:T(8,128)(2,1)S(1)}, bf16[256,4096]{1,0:T(8,128)(2,1)}, u32[]{:S(2)}) copy-start(bf16[256,4096]{1,0:T(8,128)(2,1)} %param.11) | copy-start | bytes 6291460
  337.8 6.6 %collective-permute-start.3 = (f32[256,64]{0,1:T(8,128)S(1)}, f32[256,64]{0,1:T(8,128)S(1)}, u32[]{:S(2)}, u32[]{:S(2)}) collective-permute-start(f32[256,64]{0,1:T(8,128)S(1)} %add.36), channel_id=1, source_target_pairs={{0,16},{8,24},{16,0},{24,8},{1,17},{9,25},{17,1},{25,9},{2,18},{10... | collective-permute-start | bytes 196616 | tf_op jit(solution)/shard_map/ppermute | solution.py:28
  344.4 6.4 %copy-start.6 = (f32[256,64]{0,1:T(8,128)}, f32[256,64]{0,1:T(8,128)S(1)}, u32[]{:S(2)}) copy-start(f32[256,64]{0,1:T(8,128)S(1)} %add.37) | copy-start | bytes 196612
Sparse Core Ops, SparseCore 0:
  17.2 133.3 all-reduce.2
  183.3 129.6 all-reduce.4
